TPU v7x, 768 devices: a whole 4x8x12 slice. The times are simulated.
768 devices in a mesh: grp: 48 (over z_lo, x, core), tp: 16 (over z_hi, y).
Axes of the slice: x: 4, y: 8, z: 12 (z_hi: 2, z_lo: 6; z = z_hi * 6 + z_lo), core: 2. Of those that a mesh axis runs over, the one named last changes fastest.
Arguments:
- query: bfloat16 [96, 5120], P('grp'), may hold values from -6 to 6
- key_cache: bfloat16 [96, 2048, 1024], P('grp', 'tp'), may hold values from -6 to 6
- value_cache: bfloat16 [96, 2048, 1024], P('grp', 'tp'), may hold values from -6 to 6
- lengths: int32 [96], P('grp'), may hold values from 128 to 2048
- route: int32 [96], replicated, may hold values from 0 to 95, each once
- out_weight: bfloat16 [5120, 5120], P(None, 'tp'), may hold values from -1.5 to 1.5
Outputs:
- inbox: bfloat16 [96, 5120], P('grp', 'tp')
Inputs may be any that keep to these rules, and one draw needn't show every extreme that they name: lengths are at least one block of 128 positions. `route`: every inbox row is named by exactly one trajectory.
All inputs are finite; a program needn't handle non-finite values.
Results may differ from a plain program's by a relative error of at most 0.0095.
Values may be sent and summed in bfloat16 or wider, within the bound.
A program may use at most 32 MiB of HBM per device.

v0:
```python
import jax
import jax.numpy as jnp
from jax import lax
from jax.sharding import Mesh
from jax.sharding import PartitionSpec as P

D = 5120
HEADS = 40
KV_HEADS = 8
HEAD_DIM = 128
TP = ("tp_0", "tp_1")


def all_in_one(array, axis):
    leaves = jax.tree.leaves(array)
    order = sorted(range(len(leaves)), key=lambda k: -leaves[k].size)
    width = (1, *leaves[order[0]].shape)[-1]
    lines = [
        jnp.pad(leaves[k].reshape(-1), (0, -leaves[k].size % width)).reshape(-1, width)
        for k in order
    ]
    both, at, found = (lax.all_gather(jnp.concatenate(lines), axis), 0, {})
    for k, line in zip(order, lines):
        section = both[:, at : at + len(line)].reshape(len(both), -1)
        found[k] = section[:, : leaves[k].size].reshape(-1, *leaves[k].shape)
        at += len(line)
    numbers = iter(range(len(leaves)))
    return jax.tree.map(lambda _: found[next(numbers)], array)


def combined_by_axis(array, axes, combine):
    for axis in axes:
        pieces = all_in_one(array, axis)
        array = jax.tree.map(lambda part: part[0], pieces)
        for k in range(1, lax.axis_size(axis)):
            array = combine(array, jax.tree.map(lambda part: part[k], pieces))
    return array


def sent_to_all(array, axis):
    peers = lax.axis_size(axis)
    return lax.all_to_all(
        jnp.broadcast_to(array[None], (peers, *array.shape)), axis, 0, 0, tiled=True
    )


def in_order(pieces, dim):
    shape = list(pieces.shape[1:])
    shape[dim] *= pieces.shape[0]
    return jnp.moveaxis(pieces, 0, dim).reshape(shape)


def gathered_copies(array, axis, dim):
    pieces = sent_to_all(array, axis)
    return in_order(pieces, dim)


def spread_heads(per_head):
    return jnp.repeat(per_head, HEAD_DIM, axis=1)


def body(query, key_cache, value_cache, lengths, route, out_weight):
    group = HEADS // KV_HEADS
    rows = query.shape[0]
    local_len = key_cache.shape[1]
    first = lax.axis_index(TP) * local_len
    q_heads = query.reshape(rows, KV_HEADS, group, HEAD_DIM)
    k_heads = key_cache.reshape(rows, local_len, KV_HEADS, HEAD_DIM)
    v_heads = value_cache.reshape(rows, local_len, KV_HEADS, HEAD_DIM)
    scores = jnp.einsum("bkgd,btkd->bkgt", q_heads, k_heads, preferred_element_type=jnp.float32)
    scores = scores / jnp.sqrt(jnp.float32(HEAD_DIM))
    places = first + jnp.arange(local_len, dtype=jnp.int32)
    live = (places[None, :] < lengths[:, None])[:, None, None, :]
    scores = jnp.where(live, scores, jnp.float32(-1e30))
    blockmax = jnp.max(scores, axis=3)
    expo = jnp.where(live, jnp.exp(scores - blockmax[..., None]), jnp.float32(0.0))
    blocksum = jnp.sum(expo, axis=3).reshape(rows, HEADS)
    weights = expo.astype(jnp.bfloat16)
    blockout = jnp.einsum("bkgt,btkd->bkgd", weights, v_heads, preferred_element_type=jnp.float32)
    blockout = blockout.reshape(rows, D)
    blockmax = blockmax.reshape(rows, HEADS)

    def join(left, right):
        peak = jnp.maximum(left[0], right[0])
        wleft = jnp.exp(left[0] - peak)
        wright = jnp.exp(right[0] - peak)
        return (
            peak,
            wleft * left[1] + wright * right[1],
            spread_heads(wleft) * left[2] + spread_heads(wright) * right[2],
        )

    peak, total, combined = combined_by_axis((blockmax, blocksum, blockout), TP, join)
    attended = (combined / spread_heads(total)).astype(jnp.bfloat16)
    projected = jnp.dot(attended, out_weight, preferred_element_type=jnp.float32).astype(
        jnp.bfloat16
    )
    owned = lax.axis_index("grp") * rows + jnp.arange(rows, dtype=jnp.int32)
    picker = (route[None, :] == owned[:, None]).astype(jnp.bfloat16)
    inbox = jnp.dot(
        picker, gathered_copies(projected, "grp", 0), preferred_element_type=jnp.float32
    )
    return inbox.astype(jnp.bfloat16)


def solution(mesh):
    finer = Mesh(mesh.devices.reshape(mesh.shape["grp"], 2, 8), ("grp", "tp_0", "tp_1"))
    return jax.shard_map(
        body,
        mesh=finer,
        in_specs=(
            P("grp", None),
            P("grp", TP, None),
            P("grp", TP, None),
            P("grp"),
            P(),
            P(None, TP),
        ),
        out_specs=P("grp", TP),
        check_vma=False,
    )
```

profile of v0, /device:TPU:1, one launch (start us, length us, event | category | flops | bytes accessed | tf_op | source)
XLA Modules:
  0.0 82.0 jit_solution(2772097128372888405)
XLA Ops:
  0.0 0.9 %reshape.179 = bf16[2,8,5,128]{3,2,1,0:T(8,128)(2,1)S(1)} reshape(bf16[2,5120]{1,0:T(2,128)(2,1)} %param.6) | data formatting | bytes 40960 | tf_op jit(solution)/shard_map/reshape | solution.py:67
  0.9 0.8 broadcast_compare_fusion
  1.7 1.5 %fusion.45 = (f32[2,8,5]{2,1,0:T(8,128)S(1)}, f32[2,8,5,128]{3,2,1,0:T(8,128)S(1)}) fusion(bf16[2,8,5,128]{3,2,1,0:T(8,128)(2,1)S(1)} %reshape.179, pred[2,128]{1,0:T(4,128)(4,1)S(1)} %broadcast_compare_fusion, bf16[2,128,1024]{2,1,0:T(8,128)(2,1)} %param.7), kind=kOutput, calls=%fused_computation.134 | convolution fusion | flops 2652080 | bytes 586304 | tf_op jit(solution)/shard_map/bkgd,btkd->bkgt/dot_general | solution.py:70
  3.2 0.1 reshape_reshape.7
  3.3 0.2 fusion.6
  3.5 1.3 %fusion.1 = f32[2,8,5,128]{3,2,1,0:T(8,128)S(1)} fusion(f32[2,8,5,128]{3,2,1,0:T(8,128)S(1)} %get-tuple-element.50, f32[2,8,5]{2,1,0:T(8,128)S(1)} %get-tuple-element.49, pred[2,128]{1,0:T(4,128)(4,1)S(1)} %broadcast_compare_fusion, bf16[2,128,1024]{2,1,0:T(8,128)(2,1)} %param.8), kind=kOutput, calls=%fused_computation.4 | convolution fusion | flops 2652160 | bytes 606784 | tf_op jit(solution)/shard_map/bkgt,btkd->bkgd/dot_general | solution.py:79
  4.9 0.1 reshape_reshape.8
  5.1 16.5 %all-gather.2 = f32[2,4,5120]{2,1,0:T(4,128)S(1)} all-gather(f32[1,4,5120]{2,1,0:T(4,128)S(1)} %maximum_bitcast_fusion), channel_id=2, replica_groups=mesh['grp'=48,'tp_0'=2,'tp_1'=8] {'tp_0'}, dimensions={0}, use_global_device_ids=true | all-gather | bytes 245760 | tf_op jit(solution)/shard_map/all_gather | solution.py:22
  21.7 0.1 squeeze.94
  21.8 0.1 squeeze.95
  22.1 21.3 %all-gather.3 = f32[8,4,5120]{2,1,0:T(4,128)S(1)} all-gather(f32[1,4,5120]{2,1,0:T(4,128)S(1)} %maximum_bitcast_fusion.1), channel_id=3, replica_groups=mesh['grp'=48,'tp_0'=2,'tp_1'=8] {'tp_1'}, dimensions={0}, use_global_device_ids=true | all-gather | bytes 737280 | tf_op jit(solution)/shard_map/all_gather | solution.py:22
  43.5 0.8 %copy-done.1 = f32[8,4,5120]{2,1,0:T(4,128)} copy-done((f32[8,4,5120]{2,1,0:T(4,128)}, f32[8,4,5120]{2,1,0:T(4,128)S(1)}, u32[]{:S(2)}) %copy-start.1) | copy-done | bytes 655384
  44.3 0.3 fusion.43
  44.7 0.1 squeeze.108
  44.7 0.1 squeeze.107
  44.8 0.1 squeeze.106
  44.9 0.1 squeeze.105
  45.0 0.1 squeeze.104
  45.4 0.1 squeeze.118
  47.2 2.2 %convolution_convert_fusion.1 = bf16[2,320]{1,0:T(2,128)(2,1)S(1)} fusion(bf16[5120,320]{0,1:T(8,128)(2,1)S(1)} %copy-done, f32[1,2,40,128]{3,2,1,0:T(8,128)S(1)} %broadcast_bitcast_fusion, f32[8,4,5120]{2,1,0:T(4,128)} %copy-done.1, f32[1,2,40,128]{3,2,1,0:T(8,128)S(1)} %broadcast_bitcast_fusion.1, f32[1,2,40,128]{3,2,1,0:T(8,128)S(1)} %broadcast_bitcast_fusion.2, ...), kind=kOutput, calls=%fused_computation.3 | convolution fusion | flops 6789760 | bytes 4220160 | tf_op jit(solution)/shard_map/dot_general | solution.py:95
  49.4 0.7 broadcast_in_dim.101
  50.1 20.0 %all-to-all-start = ((bf16[48,2,320]{2,1,0:T(2,128)(2,1)}), bf16[48,2,320]{2,1,0:T(2,128)(2,1)S(1)}, u32[]{:S(2)}, u32[]{:S(2)}) async-start(bf16[48,2,320]{2,1,0:T(2,128)(2,1)} %broadcast_in_dim.101), calls=%async_computation | async-start | bytes 147456 | tf_op jit(solution)/shard_map/all_to_all | solution.py:42
  70.1 11.0 %all-to-all-done = bf16[48,2,320]{2,1,0:T(2,128)(2,1)S(1)} async-done(((bf16[48,2,320]{2,1,0:T(2,128)(2,1)}), bf16[48,2,320]{2,1,0:T(2,128)(2,1)S(1)}, u32[]{:S(2)}, u32[]{:S(2)}) %all-to-all-start) | async-done | bytes 61472 | tf_op jit(solution)/shard_map/all_to_all | solution.py:42
  81.2 0.7 convolution_convert_fusion
  (54 shorter events, 2.7 us)
Async XLA Ops:
  0.0 47.2 %copy-start = (bf16[5120,320]{0,1:T(8,128)(2,1)S(1)}, bf16[5120,320]{0,1:T(8,128)(2,1)}, u32[]{:S(2)}) copy-start(bf16[5120,320]{0,1:T(8,128)(2,1)} %param.11) | copy-start | bytes 9830404
  43.5 0.8 %copy-start.1 = (f32[8,4,5120]{2,1,0:T(4,128)}, f32[8,4,5120]{2,1,0:T(4,128)S(1)}, u32[]{:S(2)}) copy-start(f32[8,4,5120]{2,1,0:T(4,128)S(1)} %all-gather.3) | copy-start | bytes 1966084
  44.3 36.9 %copy-start.2 = (s32[96]{0:T(128)S(1)}, s32[96]{0:T(128)}, u32[]{:S(2)}) copy-start(s32[96]{0:T(128)} %param.10) | copy-start | bytes 1156
  50.1 31.1 %all-to-all-start = ((bf16[48,2,320]{2,1,0:T(2,128)(2,1)}), bf16[48,2,320]{2,1,0:T(2,128)(2,1)S(1)}, u32[]{:S(2)}, u32[]{:S(2)}) async-start(bf16[48,2,320]{2,1,0:T(2,128)(2,1)} %broadcast_in_dim.101), calls=%async_computation | async-start | bytes 147456 | tf_op jit(solution)/shard_map/all_to_all | solution.py:42
where the time goes:
time: 82.3 us; the launch traced here: 82 us
  blocking collectives  37.8 us (46%)
  starting transfers between devices  20 us (24%)
  waiting for transfers between devices  11 us (13%)
  local copies, waits for them, and re-layouts  5.97 us (7%)
  matrix products  5.79 us (7%)
  other arithmetic  1.23 us (1%)
    all_gather x2, blocking collectives, all_in_one(): both, at, found = (lax.all_gather(jnp.concatenate(lines), axis), 0, {})  37.8 us
    all_to_all x1, starting transfers between devices, sent_to_all(): lax.all_to_all(jnp.broadcast_to(array[None], (peers, *array.shape)), axis...  20 us
    all_to_all x1, waiting for transfers between devices, sent_to_all(): lax.all_to_all(jnp.broadcast_to(array[None], (peers, *array.shape)), axis...  11 us
    dot_general x1, matrix products, body(): jnp.dot(attended, out_weight, preferred_element_type=jnp.float32)  2.21 us
    unnamed x26, local copies, waits for them, and re-layouts  2.17 us
  transfers between devices with their start and end apart: 1, of which 1 were waited for; matrix products, arithmetic and copies ran while one was open for 0% of the time, Pallas kernels for 0%

commit v1 on v0

v1 whole, which is shorter than its diff:
```python
import functools

import jax
import jax.numpy as jnp
from jax import lax
from jax.experimental import pallas as pl
from jax.experimental.pallas import tpu as pltpu
from jax.sharding import Mesh
from jax.sharding import PartitionSpec as P

HEADS = 40
KV_HEADS = 8
HEAD_DIM = 128
GROUP = HEADS // KV_HEADS
BLOCK = 128
NZL, NX, NC, NZH, NY = 6, 4, 2, 2, 8
NZ = NZL * NZH
PAD = 8
MESH = pl.DeviceIdType.MESH
F32 = jnp.float32
BF16 = jnp.bfloat16
TINY = 1e-30

Y_STEPS = (4, 3, 5, 2, 6, 1, 7)
Z_STEPS = (6, 5, 7, 4, 8, 3, 9, 2, 10, 1, 11)
X_STEPS = tuple((dx, dc) for dx in (2, 1, 3, 0) for dc in (1, 0) if (dx, dc) != (0, 0))
ARRIVAL = (0, 1, 7, 2, 6, 3, 5, 4)


def split3(row):
    one = row.astype(BF16).astype(F32)
    two = (row - one).astype(BF16).astype(F32)
    return one, two, row - one - two


def with_rows(tile, rows):
    at = lax.broadcasted_iota(jnp.int32, (PAD, 128), 0)
    for k, row in enumerate(rows):
        tile = jnp.where(at == GROUP + k, jnp.broadcast_to(row, (PAD, 128)), tile)
    return tile


def halves(tile):
    wide = tile.astype(F32)
    return wide[:PAD], wide[PAD:]


def kernel(
    q_hbm, k_hbm, v_hbm, w_hbm, len_ref, route_ref, out_ref,
    q_in, k_in, v_in, w_in, q_diag, part, part_got, half, half_got, give, give_got, row, row_got, pick,
    load_sem, ys_sem, yr_sem, zs_sem, zr_sem, xs_sem, xr_sem, gs_sem, gr_sem,
):
    zl, x, c = lax.axis_index("zl"), lax.axis_index("x"), lax.axis_index("c")
    zh, y = lax.axis_index("zh"), lax.axis_index("y")
    z = zh * NZL + zl

    loads = [
        pltpu.make_async_copy(src, dst, load_sem.at[n])
        for n, (src, dst) in enumerate(((q_hbm, q_in), (k_hbm, k_in), (v_hbm, v_in), (w_hbm, w_in)))
    ]
    for load in loads:
        load.start()

    def y_peer(d):
        return {"y": lax.rem(y + d, NY)}

    def z_peer(d):
        to = lax.rem(z + d, NZ)
        return {"zh": to // NZL, "zl": lax.rem(to, NZL)}

    def x_peer(dx, dc):
        return {"x": lax.rem(x + dx, NX), "c": lax.rem(c + dc, NC)}

    peers = [z_peer(d) for d in Z_STEPS] + [y_peer(d) for d in Y_STEPS] + [x_peer(*d) for d in X_STEPS]
    barrier = pltpu.get_barrier_semaphore()
    for peer in peers:
        pl.semaphore_signal(barrier, inc=1, device_id=peer, device_id_type=MESH)

    lane = lax.broadcasted_iota(jnp.int32, (1, NZL * 2 * PAD), 1)
    goes = jnp.zeros((1, NZL * 2 * PAD), jnp.int32)
    for d in range(NZL):
        from_zl = lax.rem(z - d + NZ, NZL)
        for b in range(2):
            to = route_ref[((from_zl * NX + x) * NC + c) * 2 + b]
            goes = jnp.where(lane // PAD == d * 2 + b, to, goes)
    up = lax.broadcasted_iota(jnp.int32, (NX * NC * 2 * PAD, NZL * 2 * PAD), 0)
    across = lax.broadcasted_iota(jnp.int32, (NX * NC * 2 * PAD, NZL * 2 * PAD), 1)
    slot = up // PAD
    slot_x = lax.rem(x + slot // 4, NX)
    slot_c = lax.rem(c + lax.rem(slot // 2, 2), NC)
    slot_row = ((zl * NX + slot_x) * NC + slot_c) * 2 + lax.rem(slot, 2)
    chosen = (slot_row == jnp.broadcast_to(goes, slot_row.shape)) & (lax.rem(up, PAD) == lax.rem(across, PAD))
    pick[...] = jnp.where(chosen, F32(1.0), F32(0.0)).astype(BF16)

    q_diag[...] = jnp.zeros_like(q_diag)
    loads[0].wait()
    q_wide = q_in[...].astype(F32)
    for b in range(2):
        for k in range(KV_HEADS):
            for g in range(GROUP):
                at = (k * GROUP + g) * HEAD_DIM
                to = b * KV_HEADS + k
                q_diag[to * PAD + g : to * PAD + g + 1, to * HEAD_DIM : (to + 1) * HEAD_DIM] = q_wide[
                    b : b + 1, at : at + HEAD_DIM
                ]
    q_all = q_diag[...].astype(BF16)

    loads[1].wait()
    width = KV_HEADS * HEAD_DIM
    contract = (((1,), (1,)), ((), ()))
    scores = lax.dot_general(k_in[0], q_all[:, :width], contract, preferred_element_type=F32)
    scores += lax.dot_general(k_in[1], q_all[:, width:], contract, preferred_element_type=F32)
    scores = scores * F32(HEAD_DIM**-0.5)
    place = (zh * NY + y) * BLOCK + lax.broadcasted_iota(jnp.int32, (BLOCK, 128), 0)
    length = jnp.where(lax.broadcasted_iota(jnp.int32, (BLOCK, 128), 1) < 64, len_ref[0], len_ref[1])
    live = place < length
    scores = jnp.where(live, scores, F32(-1e30))
    shift = jnp.max(scores, axis=0, keepdims=True).astype(BF16).astype(F32)
    expo = jnp.where(live, jnp.exp(scores - shift), F32(0.0))
    total = jnp.sum(expo, axis=0, keepdims=True)
    weights = expo.T.astype(BF16)
    loads[2].wait()
    outs = [jnp.dot(weights[b * 64 : b * 64 + 64], v_in[b], preferred_element_type=F32) for b in range(2)]
    total_hi, total_lo, _ = split3(total)
    for k in range(KV_HEADS):
        tiles = [o[k * PAD : (k + 1) * PAD, k * HEAD_DIM : (k + 1) * HEAD_DIM] for o in outs]
        tiles[0] = with_rows(tiles[0], (shift, total_hi, total_lo))
        part[k] = jnp.concatenate(tiles, axis=0).astype(BF16)

    pl.semaphore_wait(barrier, len(peers))

    sent = []
    for d in Y_STEPS:
        sent.append(
            pltpu.make_async_remote_copy(
                part.at[lax.rem(y + d, NY)], part_got.at[d], ys_sem.at[d], yr_sem.at[d],
                device_id=y_peer(d), device_id_type=MESH,
            )
        )
        sent[-1].start()
    got = {d: s for d, s in zip(Y_STEPS, sent)}
    tiles = []
    for d in ARRIVAL:
        if d:
            got[d].wait_recv()
        tiles.append(halves(part_got[d] if d else part[y]))
    shifts = [t[0][GROUP : GROUP + 1] for t in tiles]
    peak = functools.reduce(jnp.maximum, shifts)
    scale = [jnp.exp(s - peak) for s in shifts]
    total = sum(w * (t[0][GROUP + 1 : GROUP + 2] + t[0][GROUP + 2 : GROUP + 3]) for w, t in zip(scale, tiles))
    total = jnp.maximum(total, F32(TINY))
    down = lax.broadcasted_iota(jnp.int32, (PAD, 128), 0)
    right = lax.broadcasted_iota(jnp.int32, (PAD, 128), 1)
    mine = [right == b * 64 + y * PAD + down for b in range(2)]

    def column(line, b):
        return jnp.sum(jnp.where(mine[b], jnp.broadcast_to(line, (PAD, 128)), F32(0.0)), axis=1, keepdims=True)

    mixed = []
    for b in range(2):
        mixed.append(sum(column(w / total, b) * t[b] for w, t in zip(scale, tiles)))
    mixed[0] = with_rows(mixed[0], split3(peak + jnp.log(total)))
    half[...] = jnp.concatenate(mixed, axis=0).astype(BF16)

    got = {}
    for d in Z_STEPS:
        got[d] = pltpu.make_async_remote_copy(
            half, half_got.at[d], zs_sem.at[d], zr_sem.at[d], device_id=z_peer(d), device_id_type=MESH
        )
        got[d].start()
        sent.append(got[d])
    held = [None] * NZL
    for d in (0, 1, 5, 2, 4, 3):
        ends = []
        for e in (d, d + NZL):
            if e:
                got[e].wait_recv()
            ends.append(halves(half_got[e] if e else half[...]))
        logs = [jnp.sum(t[0][GROUP:], axis=0, keepdims=True) for t in ends]
        top = jnp.maximum(logs[0], logs[1])
        es = [jnp.exp(v - top) for v in logs]
        share = es[0] / (es[0] + es[1])
        both = []
        for b in range(2):
            part0 = column(share, b)
            both.append(part0 * ends[0][b] + (F32(1.0) - part0) * ends[1][b])
        held[d] = jnp.concatenate(both, axis=0).astype(BF16)
    rows = jnp.concatenate(held, axis=0)
    give[...] = jnp.dot(pick[...], rows, preferred_element_type=F32).astype(BF16).reshape(give.shape)

    got = {}
    for dx, dc in X_STEPS:
        n = dx * NC + dc
        got[n] = pltpu.make_async_remote_copy(
            give.at[n], give_got.at[n], xs_sem.at[n], xr_sem.at[n], device_id=x_peer(dx, dc), device_id_type=MESH
        )
        got[n].start()
        sent.append(got[n])
    whole = give[0].astype(F32)
    for n in (1, 2, 3, 6, 7, 4, 5):
        got[n].wait_recv()
        whole += give_got[n].astype(F32)
    row[...] = whole.astype(BF16)

    got = {}
    for d in Y_STEPS:
        got[d] = pltpu.make_async_remote_copy(
            row, row_got.at[d], gs_sem.at[d], gr_sem.at[d], device_id=y_peer(d), device_id_type=MESH
        )
        got[d].start()
        sent.append(got[d])
    loads[3].wait()
    answer = None
    for d in ARRIVAL:
        if d:
            got[d].wait_recv()
        pieces = halves(row_got[d] if d else row[...])
        spread = jnp.concatenate(
            [
                jnp.concatenate([jnp.where(down == g, t, F32(0.0)) for t in pieces], axis=0)
                for g in range(GROUP)
            ],
            axis=1,
        ).astype(BF16)
        first = pl.multiple_of(lax.rem(y - d + NY, NY) * (GROUP * HEAD_DIM), 128)
        some = lax.dot_general(
            w_in[:, pl.ds(first, GROUP * HEAD_DIM)], spread, contract, preferred_element_type=F32
        )
        answer = some if answer is None else answer + some
    answer = answer.T
    out_ref[...] = jnp.concatenate(
        [jnp.sum(answer[i * PAD : (i + 1) * PAD], axis=0, keepdims=True) for i in range(2)], axis=0
    ).astype(BF16)
    for copy in sent:
        copy.wait_send()


def body(query, key_cache, value_cache, lengths, route, out_weight):
    tile = (2 * PAD, HEAD_DIM)
    rows, width = query.shape[0], out_weight.shape[1]
    anywhere = pl.BlockSpec(memory_space=pl.ANY)
    scalars = pl.BlockSpec(memory_space=pltpu.SMEM)
    sems = pltpu.SemaphoreType.DMA
    return pl.pallas_call(
        kernel,
        out_shape=jax.ShapeDtypeStruct((rows, width), BF16),
        in_specs=[anywhere] * 4 + [scalars] * 2,
        out_specs=pl.BlockSpec(memory_space=pltpu.VMEM),
        scratch_shapes=[
            pltpu.VMEM(query.shape, BF16),
            pltpu.VMEM(key_cache.shape, BF16),
            pltpu.VMEM(value_cache.shape, BF16),
            pltpu.VMEM(out_weight.shape[::-1], BF16),
            pltpu.VMEM((128, 2 * KV_HEADS * HEAD_DIM), F32),
            pltpu.VMEM((KV_HEADS, *tile), BF16),
            pltpu.VMEM((NY, *tile), BF16),
            pltpu.VMEM(tile, BF16),
            pltpu.VMEM((NZ, *tile), BF16),
            pltpu.VMEM((NX * NC, *tile), BF16),
            pltpu.VMEM((NX * NC, *tile), BF16),
            pltpu.VMEM(tile, BF16),
            pltpu.VMEM((NY, *tile), BF16),
            pltpu.VMEM((NX * NC * 2 * PAD, NZL * 2 * PAD), BF16),
            sems((4,)),
            sems((NY,)), sems((NY,)),
            sems((NZ,)), sems((NZ,)),
            sems((NX * NC,)), sems((NX * NC,)),
            sems((NY,)), sems((NY,)),
        ],
        compiler_params=pltpu.CompilerParams(collective_id=0, has_side_effects=True),
    )(query, key_cache, value_cache, out_weight.T, lengths, route)


def solution(mesh):
    finer = Mesh(mesh.devices.reshape(NZL, NX, NC, NZH, NY), ("zl", "x", "c", "zh", "y"))
    grp, tp = ("zl", "x", "c"), ("zh", "y")
    return jax.shard_map(
        body,
        mesh=finer,
        in_specs=(
            P(grp, None),
            P(grp, tp, None),
            P(grp, tp, None),
            P(grp),
            P(),
            P(None, tp),
        ),
        out_specs=P(grp, tp),
        check_vma=False,
    )
```

time: 82.3 us -> 42.6 us (0.52)
  Pallas kernels: 0 us -> 41.2 us
  blocking collectives: 37.8 us -> 0 us
  starting transfers between devices: 20 us -> 0 us
  waiting for transfers between devices: 11 us -> 0 us
  matrix products: 5.79 us -> 0 us
  local copies, waits for them, and re-layouts: 5.97 us -> 1.25 us
  other arithmetic: 1.23 us -> 0 us
    pallas_call x0 -> x1, Pallas kernels: none -> 41.2 us  [body(): pl.pallas_call(kernel, out_shape=jax.ShapeDtypeStruct((rows, width), BF16...]
    all_gather x2 -> x0, blocking collectives: 37.8 us -> none  [all_in_one(): both, at, found = (lax.all_gather(jnp.concatenate(lines), axis), 0, {})]
    all_to_all x1 -> x0, starting transfers between devices: 20 us -> none  [sent_to_all(): lax.all_to_all(jnp.broadcast_to(array[None], (peers, *array.shape)), axis...]
    all_to_all x1 -> x0, waiting for transfers between devices: 11 us -> none  [sent_to_all(): lax.all_to_all(jnp.broadcast_to(array[None], (peers, *array.shape)), axis...]
    dot_general x4 -> x0, matrix products: 5.79 us -> none  [the longest x1 2.21 us: body(): jnp.dot(attended, out_weight, preferred_element_type=jnp.float32)]
    squeeze x18 -> x0, local copies, waits for them, and re-layouts: 1.46 us -> none  [the longest x15 1.22 us: combined_by_axis(): array = combine(array, jax.tree.map(lambda part: part[k], pieces))]
    reshape x3 -> x0, local copies, waits for them, and re-layouts: 1.01 us -> none  [the longest x1 0.91 us: body(): q_heads = query.reshape(rows, KV_HEADS, group, HEAD_DIM)]
    unnamed x26 -> x1, local copies, waits for them, and re-layouts: 2.17 us -> 1.25 us
  transfers between devices with their start and end apart: 1 -> 0, of which waited for: 1 -> 0; matrix products, arithmetic and copies ran while one was open for 0% -> 0% of each run, Pallas kernels for 0% -> 0%
where the time goes in v1:
time: 42.6 us; the launch traced here: 42.4 us
  Pallas kernels  41.2 us (97%)
  local copies, waits for them, and re-layouts  1.25 us (3%)
    pallas_call x1, Pallas kernels, body(): pl.pallas_call(kernel, out_shape=jax.ShapeDtypeStruct((rows, width), BF16...  41.2 us
    unnamed x1, local copies, waits for them, and re-layouts  1.25 us

profile of v1, /device:TPU:1, one launch (start us, length us, event | category | flops | bytes accessed | tf_op | source)
XLA Modules:
  0.0 42.4 jit_solution(12444086467632813150)
XLA Ops:
  0.0 41.2 %shard_map.64 = bf16[2,320]{1,0:T(2,128)(2,1)} custom-call(bf16[2,5120]{1,0:T(2,128)(2,1)} %q_hbm.1, bf16[2,128,1024]{2,1,0:T(8,128)(2,1)} %k_hbm.1, bf16[2,128,1024]{2,1,0:T(8,128)(2,1)} %v_hbm.1, bf16[320,5120]{1,0:T(8,128)(2,1)} %bitcast.1, s32[2]{0:T(128)} %len_ref.1, s32[96]{0:T(128)} %route_ref.1), custom_call_target="tpu_custom_call" | custom-call | tf_op jit(solution)/shard_map/pallas_call | solution.py:244
  41.2 1.2 %copy.8 = bf16[2,320]{1,0:T(2,128)(2,1)} copy(bf16[2,320]{1,0:T(2,128)(2,1)} %shard_map.64) | data formatting | bytes 2560
